TPU v7x, 128 devices: a whole 4x4x4 slice. The times are simulated.
128 devices in a mesh: dp: 2 (over core), seq: 16 (over y, x), tensor: 4 (over z).
Axes of the slice: x: 4, y: 4, z: 4, core: 2. Of those that a mesh axis runs over, the one named last changes fastest.
Arguments:
- tokens: bfloat16 [2, 8192, 2048], P('dp', ('seq', 'tensor')), may hold values from -6 to 6
- attn_gain: float32 [2048], replicated, may hold values from 0.5 to 1.5
- w_qkv: bfloat16 [3, 2048, 2048], P(None, None, 'tensor'), may hold values from -1 to 1
- w_out: bfloat16 [2048, 2048], P('tensor'), may hold values from -0.125 to 0.125
- mlp_gain: float32 [2048], replicated, may hold values from 0.5 to 1.5
- w_up: bfloat16 [2048, 8192], P(None, 'tensor'), may hold values from -0.125 to 0.125
- w_down: bfloat16 [8192, 2048], P('tensor'), may hold values from -0.0625 to 0.0625
- pool_gain: float32 [2048], replicated, may hold values from -8 to 8
- pool_bias: float32 [2048], replicated, may hold values from 0.5 to 5
- value_weight: float32 [2048], replicated, may hold values from -6 to 6
- valid_frames: int32 [2], replicated, may hold values from 16 to 32, as said below
Outputs:
- hidden: bfloat16 [2, 8192, 2048], P('dp', ('seq', 'tensor'))
- frame_values: float32 [2, 32], P('dp', 'seq')
- advantages: float32 [2, 32], P('dp', 'seq')
Inputs may be any that keep to these rules, and one draw needn't show every extreme that they name: `valid_frames`: at least one rollout keeps all 32 frames and at least one keeps 32 // 2 of them.
All inputs are finite; a program needn't handle non-finite values.
Results may differ from a plain program's by a relative error of at most 0.017.
Values may be sent and summed in bfloat16 or wider, within the bound.
A program may use at most 256 MiB of HBM per device.

v0:
```python
import jax
import jax.numpy as jnp
from jax import lax
from jax.sharding import PartitionSpec as P

HEAD_DIM = 128
TOK_FRAME = 256
FR_DEV = 2


def laid_out(blocks, dim):
    shape = list(blocks.shape[1:])
    shape[dim] *= blocks.shape[0]
    return jnp.moveaxis(blocks, 0, dim).reshape(shape)


def sent_to_all(array, axis):
    copies = jnp.broadcast_to(array, (lax.axis_size(axis), *array.shape))
    return lax.all_to_all(copies, axis, split_axis=0, concat_axis=0, tiled=True)


def gathered_copies(array, axis, dim):
    return laid_out(sent_to_all(array, axis), dim)


def cut_along(array, dim, size):
    shape = array.shape
    blocks = array.reshape(*shape[:dim], size, shape[dim] // size, *shape[dim + 1 :])
    return jnp.moveaxis(blocks, dim, 0)


def summed_on_arrival(array, axis, dim):
    size = lax.axis_size(axis)
    blocks = lax.all_to_all(cut_along(array, dim, size), axis, 0, 0, tiled=True)
    return jnp.sum(blocks.astype(jnp.float32), axis=0)


def over_copies(array, axis):
    everything = sent_to_all(array, axis)
    return jnp.sum(everything, axis=0)


def collected_together(array, axis):
    leaves = jax.tree.leaves(array)
    sequence = sorted(range(len(leaves)), key=lambda k: -leaves[k].size)
    width = (1, *leaves[sequence[0]].shape)[-1]
    lines = [
        jnp.pad(leaves[k].reshape(-1), (0, -leaves[k].size % width)).reshape(-1, width)
        for k in sequence
    ]
    both, at, found = (sent_to_all(jnp.concatenate(lines), axis), 0, {})
    for k, line in zip(sequence, lines):
        piece = both[:, at : at + len(line)].reshape(len(both), -1)
        found[k] = piece[:, : leaves[k].size].reshape(-1, *leaves[k].shape)
        at += len(line)
    numbers = iter(range(len(leaves)))
    return jax.tree.map(lambda _: found[next(numbers)], array)


def combined_pairwise(pieces, combine):
    while len(jax.tree.leaves(pieces)[0]) > 1:
        pieces = jax.vmap(combine)(
            *(jax.tree.map(lambda part: part[side::2], pieces) for side in (0, 1))
        )
    return jax.tree.map(lambda part: part[0], pieces)


def entering_2(array, axis, combine, identity):
    size, index = (lax.axis_size(axis), lax.axis_index(axis))
    passed = jnp.arange(size) < index

    def kept(part, zero, own):
        part = jnp.where(
            passed.reshape(-1, *(1 for _ in own.shape)), part, jnp.asarray(zero, own.dtype)
        )
        return part

    pieces = collected_together(array, axis)
    return combined_pairwise(jax.tree.map(kept, pieces, identity, array), combine)


def rms_norm(values, gain):
    floats = values.astype(jnp.float32)
    square = jnp.mean(floats * floats, axis=-1, keepdims=True)
    return (floats * lax.rsqrt(square + 1e-05) * gain).astype(jnp.bfloat16)


def compose(earlier, later):
    return (earlier[0] * later[0], later[0] * earlier[1] + later[1])


def local(
    tokens,
    attn_gain,
    w_qkv,
    w_out,
    mlp_gain,
    w_up,
    w_down,
    pool_gain,
    pool_bias,
    value_weight,
    valid_frames,
):
    rows = tokens[0]
    row_count = rows.shape[0]
    seq_index = lax.axis_index("seq")
    tensor_index = lax.axis_index("tensor")
    roll_index = lax.axis_index("dp")
    length = valid_frames[roll_index]
    local_heads = w_qkv.shape[2] // HEAD_DIM
    scale = 1.0 / HEAD_DIM**0.5
    normed = rms_norm(rows, attn_gain)
    qkv = jnp.einsum(
        "nd,cde->nce",
        gathered_copies(normed, "tensor", 0),
        w_qkv,
        preferred_element_type=jnp.float32,
    ).astype(jnp.bfloat16)
    block = qkv.shape[0]
    query = qkv[:, 0].reshape(block, local_heads, HEAD_DIM)
    query_frame = (seq_index * block + jnp.arange(block, dtype=jnp.int32)) // TOK_FRAME
    peak = jnp.full((local_heads, block), -1e30, jnp.float32)
    key_piece = lax.all_gather(qkv[:, 1], "seq", axis=0, tiled=True)
    value_piece = lax.all_gather(qkv[:, 2], "seq", axis=0, tiled=True)
    width = key_piece.shape[0]
    key_heads = key_piece.reshape(width, local_heads, HEAD_DIM)
    value_heads = value_piece.reshape(width, local_heads, HEAD_DIM)
    scores = (
        jnp.einsum("qhe,khe->hqk", query, key_heads, preferred_element_type=jnp.float32) * scale
    )
    key_frame = jnp.arange(width, dtype=jnp.int32) // TOK_FRAME
    allowed = (key_frame[None, :] <= query_frame[:, None]) & (key_frame[None, :] < length)
    scores = jnp.where(allowed[None], scores, -1e30)
    new_peak = jnp.maximum(peak, jnp.max(scores, axis=-1))
    weights = jnp.where(allowed[None], jnp.exp(scores - new_peak[..., None]), 0.0)
    total = jnp.sum(weights, axis=-1)
    acc = jnp.einsum(
        "hqk,khe->hqe",
        weights.astype(jnp.bfloat16),
        value_heads,
        preferred_element_type=jnp.float32,
    )
    peak, total, acc = (new_peak, total, acc)
    mixed = (
        (acc / total[..., None])
        .transpose(1, 0, 2)
        .reshape(block, local_heads * HEAD_DIM)
        .astype(jnp.bfloat16)
    )
    attn_sum = summed_on_arrival(
        jnp.dot(mixed, w_out, preferred_element_type=jnp.float32).astype(jnp.bfloat16), "tensor", 0
    )
    after_attn = (rows.astype(jnp.float32) + attn_sum).astype(jnp.bfloat16)
    normed2 = rms_norm(after_attn, mlp_gain)
    up = jax.nn.gelu(
        jnp.dot(gathered_copies(normed2, "tensor", 0), w_up, preferred_element_type=jnp.float32),
        approximate=True,
    ).astype(jnp.bfloat16)
    down_sum = summed_on_arrival(
        jnp.dot(up, w_down, preferred_element_type=jnp.float32).astype(jnp.bfloat16), "tensor", 0
    )
    hidden = (after_attn.astype(jnp.float32) + down_sum).astype(jnp.bfloat16)
    local_frame = (tensor_index * row_count + jnp.arange(row_count, dtype=jnp.int32)) // TOK_FRAME
    selector = (local_frame[None, :] == jnp.arange(FR_DEV, dtype=jnp.int32)[:, None]).astype(
        jnp.bfloat16
    )
    sums = jnp.dot(selector, hidden, preferred_element_type=jnp.float32)
    sums = over_copies(sums, "tensor")
    gain, offset, head_weight = (pool_gain, pool_bias, value_weight)
    means = sums / TOK_FRAME
    frame_global = seq_index * FR_DEV + jnp.arange(FR_DEV, dtype=jnp.int32)
    valid = frame_global < length
    gate = jax.nn.sigmoid(means * gain + offset)
    decay = jnp.where(valid[:, None], gate, 1.0)
    source = jnp.where(valid[:, None], (1.0 - gate) * means, 0.0)
    agg_decay = jnp.ones_like(means[0])
    agg_source = jnp.zeros_like(means[0])
    for frame in range(FR_DEV):
        agg_decay, agg_source = compose((agg_decay, agg_source), (decay[frame], source[frame]))
    entering = entering_2(
        (agg_decay, agg_source),
        "seq",
        compose,
        (jnp.ones_like(agg_decay), jnp.zeros_like(agg_source)),
    )
    state = entering[1]
    collected = []
    for frame in range(FR_DEV):
        state = decay[frame] * state + source[frame]
        collected.append(jnp.sum(state * head_weight))
    partial_values = jnp.stack(collected)
    values = jnp.where(valid, partial_values, 0.0)
    pick = jnp.sum(jnp.where(frame_global == length - 1, values, 0.0))
    count = jnp.sum(valid_frames).astype(jnp.float32)
    slot = (jnp.arange(lax.axis_size("dp"), dtype=jnp.int32) == roll_index).astype(jnp.float32)
    entries = jnp.stack([pick, jnp.sum(values), jnp.sum(values * values)])
    table = over_copies(entries[:, None] * slot[None, :], ("dp", "seq"))
    finals, first_sums, second_sums = (table[0], table[1], table[2])
    lengths = valid_frames.astype(jnp.float32)
    mean = jnp.sum(lengths * finals - first_sums) / count
    squares = jnp.sum(lengths * finals * finals - 2.0 * finals * first_sums + second_sums) / count
    variance = squares - mean * mean
    final = jnp.sum(finals * slot)
    gap = jnp.where(valid, final - values, 0.0)
    centered = jnp.where(valid, gap - mean, 0.0)
    advantages = jnp.where(valid, centered * lax.rsqrt(variance + 1e-05), 0.0)
    return (hidden[None], values[None], advantages[None])


def solution(mesh):
    in_specs = (
        P("dp", ("seq", "tensor"), None),
        P(),
        P(None, None, "tensor"),
        P("tensor", None),
        P(),
        P(None, "tensor"),
        P("tensor", None),
        P(),
        P(),
        P(),
        P(),
    )
    out_specs = (P("dp", ("seq", "tensor"), None), P("dp", "seq"), P("dp", "seq"))
    return jax.shard_map(local, mesh=mesh, in_specs=in_specs, out_specs=out_specs, check_vma=False)
```

profile of v0, /device:TPU:1, one launch (start us, length us, event | category | flops | bytes accessed | tf_op | source)
XLA Modules:
  0.0 397.9 jit_solution(1395034552048912833)
XLA Ops:
  7.2 1.4 fusion.25
  8.6 1.7 fusion.27
  10.6 31.1 %all_to_all.35 = bf16[4,128,2048]{2,1,0:T(8,128)(2,1)S(1)} all-to-all(bf16[4,128,2048]{2,1,0:T(8,128)(2,1)S(1)} %broadcast_in_dim.104), channel_id=1, replica_groups=mesh['dp'=2,'seq'=16,'tensor'=4] {'tensor'}, dimensions={0} | all-to-all | bytes 4194304 | tf_op jit(solution)/shard_map/all_to_all | solution.py:19
  41.7 3.5 convolution_convert_fusion.2
  45.2 1.1 fusion.63
  48.3 4.9 %compare_and_fusion = pred[512,8192]{1,0:T(8,128)(4,1)} fusion(s32[8192]{0:T(1024)S(1)} %add_select_fusion, s32[512]{0:T(512)S(1)} %add_select_fusion.1, pred[8192]{0:T(1024)(128)(4,1)S(1)} %broadcast_compare_fusion), kind=kLoop, calls=%fused_computation.7 | loop fusion | flops 8388608 | bytes 4237312 | tf_op jit(solution)/shard_map/and | solution.py:133
  53.2 69.6 %all-gather.5.cloned.1.call-done = bf16[8192,1,512]{0,2,1:T(8,128)(2,1)} async-done(((bf16[512,1,512]{0,2,1:T(8,128)(2,1)}), bf16[8192,1,512]{0,2,1:T(8,128)(2,1)}) %all-gather.5.cloned.1.call-update) | async-done | bytes 8388624 | tf_op jit(solution)/shard_map/all_gather | solution.py:124
  122.8 30.0 %fusion = (f32[4,512]{1,0:T(4,128)S(1)}, f32[4,512,8192]{2,1,0:T(8,128)}) fusion(pred[512,8192]{1,0:T(8,128)(4,1)} %compare_and_fusion, bf16[512,4,128]{0,2,1:T(8,128)(2,1)S(1)} %bitcast.73, bf16[8192,4,128]{0,2,1:T(8,128)(2,1)} %bitcast.78), kind=kOutput, calls=%fused_computation.2 | convolution fusion | flops 4345296896 | bytes 80224256 | tf_op jit(solution)/shard_map/qhe,khe->hqk/dot_general | solution.py:130
  152.8 23.6 %fusion.1 = f32[4,512]{1,0:T(4,128)S(1)} fusion(f32[4,512,8192]{2,1,0:T(8,128)} %get-tuple-element.36, f32[4,512]{1,0:T(4,128)S(1)} %broadcast_maximum_fusion, pred[512,8192]{1,0:T(8,128)(4,1)} %compare_and_fusion), kind=kLoop, calls=%fused_computation.3 | loop fusion | flops 83884032 | bytes 71319552 | tf_op jit(solution)/shard_map/reduce_sum | solution.py:137
  176.4 25.0 %all-gather.7.cloned.1.call-done = bf16[8192,1,512]{0,2,1:T(8,128)(2,1)} async-done(((bf16[512,1,512]{0,2,1:T(8,128)(2,1)}), bf16[8192,1,512]{0,2,1:T(8,128)(2,1)}) %all-gather.7.cloned.1.call-update) | async-done | bytes 8388624 | tf_op jit(solution)/shard_map/all_gather | solution.py:125
  201.4 28.9 %divide_convert_fusion = bf16[512,4,128]{0,2,1:T(8,128)(2,1)S(1)} fusion(bf16[8192,4,128]{0,2,1:T(8,128)(2,1)} %bitcast.79, f32[4,512,8192]{2,1,0:T(8,128)} %get-tuple-element.36, f32[4,512]{1,0:T(4,128)S(1)} %broadcast_maximum_fusion, pred[512,8192]{1,0:T(8,128)(4,1)} %compare_and_fusion, f32[512,4]{0,1:T(4,128)S(1)} %bitcast.77), kind=kOutput, calls=%fused_computation.46 | convolution fusion | flops 4379377664 | bytes 80232448 | tf_op jit(solution)/shard_map/hqk,khe->hqe/dot_general | solution.py:138
  230.4 1.3 convolution_convert_fusion.1
  231.7 28.0 %all_to_all.36 = bf16[4,128,2048]{2,1,0:T(8,128)(2,1)S(1)} all-to-all(bf16[4,128,2048]{2,1,0:T(8,128)(2,1)S(1)} %bitcast.71), channel_id=1, replica_groups=mesh['dp'=2,'seq'=16,'tensor'=4] {'tensor'}, dimensions={0} | all-to-all | bytes 4194304 | tf_op jit(solution)/shard_map/all_to_all | solution.py:34
  261.6 26.4 %all_to_all.37 = bf16[4,128,2048]{2,1,0:T(8,128)(2,1)} all-to-all(bf16[4,128,2048]{2,1,0:T(8,128)(2,1)S(1)} %broadcast_in_dim.108), channel_id=1, replica_groups=mesh['dp'=2,'seq'=16,'tensor'=4] {'tensor'}, dimensions={0} | all-to-all | bytes 4194304 | tf_op jit(solution)/shard_map/all_to_all | solution.py:19
  288.0 16.6 %convolution_convert_fusion = bf16[512,2048]{1,0:T(8,128)(2,1)} fusion(bf16[2048,2048]{1,0:T(8,128)(2,1)} %param.17, bf16[512,2048]{1,0:T(8,128)(2,1)} %bitcast.72, bf16[2048,2048]{1,0:T(8,128)(2,1)} %param.16), kind=kOutput, calls=%fused_computation.19 | convolution fusion | flops 8600420352 | bytes 20971520 | tf_op jit(solution)/shard_map/dot_general | solution.py:161
  304.6 4.6 %all-to-all-start.3 = ((bf16[4,128,2048]{2,1,0:T(8,128)(2,1)}), bf16[4,128,2048]{2,1,0:T(8,128)(2,1)}, u32[]{:S(2)}, u32[]{:S(2)}) async-start(bf16[4,128,2048]{2,1,0:T(8,128)(2,1)} %bitcast.69), calls=%async_computation.3 | async-start | bytes 4194304 | tf_op jit(solution)/shard_map/all_to_all | solution.py:34
  309.2 22.3 %all-to-all-done.3 = bf16[4,128,2048]{2,1,0:T(8,128)(2,1)} async-done(((bf16[4,128,2048]{2,1,0:T(8,128)(2,1)}), bf16[4,128,2048]{2,1,0:T(8,128)(2,1)}, u32[]{:S(2)}, u32[]{:S(2)}) %all-to-all-start.3) | async-done | bytes 2097184 | tf_op jit(solution)/shard_map/all_to_all | solution.py:34
  331.5 2.1 convert_reduce_fusion
  333.7 1.0 copy-done.1
  334.6 1.3 fusion.37
  336.6 3.3 all-to-all-start.4
  340.5 3.8 all-to-all-done.4
  345.9 4.7 %all-to-all-start.5 = ((f32[16,2,2048]{2,1,0:T(2,128)}), f32[16,2,2048]{2,1,0:T(2,128)S(1)}, u32[]{:S(2)}, u32[]{:S(2)}) async-start(f32[16,2,2048]{2,1,0:T(2,128)} %broadcast_in_dim.113), calls=%async_computation.5 | async-start | bytes 524288 | tf_op jit(solution)/shard_map/all_to_all | solution.py:19
  353.1 5.0 %all-to-all-done.5 = f32[16,2,2048]{2,1,0:T(2,128)S(1)} async-done(((f32[16,2,2048]{2,1,0:T(2,128)}), f32[16,2,2048]{2,1,0:T(2,128)S(1)}, u32[]{:S(2)}, u32[]{:S(2)}) %all-to-all-start.5) | async-done | bytes 262176 | tf_op jit(solution)/shard_map/all_to_all | solution.py:19
  359.7 1.4 multiply_reduce_fusion.1
  361.1 2.5 fusion.52
  363.6 2.0 pad_maximum_fusion.1
  366.9 11.1 %all-to-all-start.6 = ((f32[32,3,2]{1,2,0:T(2,128)}), f32[32,3,2]{1,2,0:T(2,128)S(1)}, u32[]{:S(2)}, u32[]{:S(2)}) async-start(f32[32,3,2]{1,2,0:T(2,128)} %broadcast_in_dim.118), calls=%async_computation.6 | async-start | bytes 65536 | tf_op jit(solution)/shard_map/all_to_all | solution.py:19
  378.1 2.3 fusion.34
  380.4 4.7 %all-to-all-done.6 = f32[32,3,2]{1,2,0:T(2,128)S(1)} async-done(((f32[32,3,2]{1,2,0:T(2,128)}), f32[32,3,2]{1,2,0:T(2,128)S(1)}, u32[]{:S(2)}, u32[]{:S(2)}) %all-to-all-start.6) | async-done | bytes 800 | tf_op jit(solution)/shard_map/all_to_all | solution.py:19
  385.3 1.4 subtract_reduce_fusion
  388.0 3.1 multiply_select_fusion.2
  (70 shorter events, 11.4 us)
Async XLA Ops:
  7.2 223.2 %copy-start = (bf16[512,2048]{1,0:T(8,128)(2,1)S(1)}, bf16[512,2048]{1,0:T(8,128)(2,1)}, u32[]{:S(2)}) copy-start(bf16[512,2048]{1,0:T(8,128)(2,1)} %param.14) | copy-start | bytes 6291460
  7.2 115.6 %all-gather.5.cloned.1.call-start = ((), (), s32[]{:S(2)}) async-start(), calls=%async_computation.7 | async-start | bytes 8912896 | tf_op jit(solution)/shard_map/all_gather | solution.py:124
  7.2 34.5 %copy-start.9 = (bf16[3,2048,512]{2,1,0:T(8,128)(2,1)S(1)}, bf16[3,2048,512]{2,1,0:T(8,128)(2,1)}, u32[]{:S(2)}) copy-start(bf16[3,2048,512]{2,1,0:T(8,128)(2,1)} %param.13) | copy-start | bytes 18874372
  41.7 5.3 %copy-start.8 = (s32[2]{0:T(128)S(1)}, s32[2]{0:T(128)}, u32[]{:S(2)}) copy-start(s32[2]{0:T(128)} %param.21) | copy-start | bytes 28
  46.3 155.1 %all-gather.7.cloned.1.call-start = ((), (), s32[]{:S(2)}) async-start(), calls=%async_computation.8 | async-start | bytes 8912896 | tf_op jit(solution)/shard_map/all_gather | solution.py:125
  230.4 29.7 %copy-start.2 = (bf16[1,128,2048]{2,1,0:T(8,128)(2,1)S(1)}, bf16[1,128,2048]{2,1,0:T(8,128)(2,1)}, u32[]{:S(2)}) copy-start(bf16[1,128,2048]{2,1,0:T(8,128)(2,1)} %param.11) | copy-start | bytes 1572868
  230.4 30.7 %copy-start.5 = (f32[2048]{0:T(1024)S(1)}, f32[2048]{0:T(1024)}, u32[]{:S(2)}) copy-start(f32[2048]{0:T(1024)} %param.15) | copy-start | bytes 24580
  260.3 0.8 copy-start.3
  288.0 21.2 %copy-start.6 = (f32[2048]{0:T(1024)S(1)}, f32[2048]{0:T(1024)}, u32[]{:S(2)}) copy-start(f32[2048]{0:T(1024)} %param.18) | copy-start | bytes 24580
  304.6 39.8 %copy-start.7 = (f32[2048]{0:T(1024)S(1)}, f32[2048]{0:T(1024)}, u32[]{:S(2)}) copy-start(f32[2048]{0:T(1024)} %param.19) | copy-start | bytes 24580
  304.6 27.0 %all-to-all-start.3 = ((bf16[4,128,2048]{2,1,0:T(8,128)(2,1)}), bf16[4,128,2048]{2,1,0:T(8,128)(2,1)}, u32[]{:S(2)}, u32[]{:S(2)}) async-start(bf16[4,128,2048]{2,1,0:T(8,128)(2,1)} %bitcast.69), calls=%async_computation.3 | async-start | bytes 4194304 | tf_op jit(solution)/shard_map/all_to_all | solution.py:34
  333.7 1.0 copy-start.1
  336.6 7.7 %all-to-all-start.4 = ((f32[4,2,2048]{2,1,0:T(2,128)}), f32[4,2,2048]{2,1,0:T(2,128)S(1)}, u32[]{:S(2)}, u32[]{:S(2)}) async-start(f32[4,2,2048]{2,1,0:T(2,128)} %broadcast_in_dim.110), calls=%async_computation.4 | async-start | bytes 131072 | tf_op jit(solution)/shard_map/all_to_all | solution.py:19
  344.4 1.5 copy-start.4
  345.9 12.2 %all-to-all-start.5 = ((f32[16,2,2048]{2,1,0:T(2,128)}), f32[16,2,2048]{2,1,0:T(2,128)S(1)}, u32[]{:S(2)}, u32[]{:S(2)}) async-start(f32[16,2,2048]{2,1,0:T(2,128)} %broadcast_in_dim.113), calls=%async_computation.5 | async-start | bytes 524288 | tf_op jit(solution)/shard_map/all_to_all | solution.py:19
  366.9 18.1 %all-to-all-start.6 = ((f32[32,3,2]{1,2,0:T(2,128)}), f32[32,3,2]{1,2,0:T(2,128)S(1)}, u32[]{:S(2)}, u32[]{:S(2)}) async-start(f32[32,3,2]{1,2,0:T(2,128)} %broadcast_in_dim.118), calls=%async_computation.6 | async-start | bytes 65536 | tf_op jit(solution)/shard_map/all_to_all | solution.py:19
Sparse Core Ops, SparseCore 0:
  46.4 76.3 all-gather.4
  124.9 76.4 all-gather.6
where the time goes:
time: 399 us; the launch traced here: 398 us
  waiting for transfers between devices  131 us (33%)
  blocking collectives  85.5 us (21%)
  matrix products  81.5 us (20%)
  other arithmetic  52.2 us (13%)
  starting transfers between devices  23.7 us (6%)
  between operations  17 us (4%)
  local copies, waits for them, and re-layouts  6.76 us (2%)
    all_gather x1, waiting for transfers between devices, local(): key_piece = lax.all_gather(qkv[:, 1], 'seq', axis=0, tiled=True)  69.6 us
    all_to_all x2, blocking collectives, sent_to_all(): return lax.all_to_all(copies, axis, split_axis=0, concat_axis=0, tiled=True)  57.6 us
    dot_general x1, matrix products, local(): jnp.einsum('qhe,khe->hqk', query, key_heads, preferred_element_type=jnp.f...  30 us
    dot_general x1, matrix products, local(): jnp.einsum('hqk,khe->hqe', weights.astype(jnp.bfloat16), value_heads, pre...  28.9 us
    all_to_all x1, blocking collectives, summed_on_arrival(): blocks = lax.all_to_all(cut_along(array, dim, size), axis, 0, 0, tiled=True)  28 us
    all_gather x1, waiting for transfers between devices, local(): value_piece = lax.all_gather(qkv[:, 2], 'seq', axis=0, tiled=True)  25 us
    reduce_sum x1, other arithmetic, local(): total = jnp.sum(weights, axis=-1)  23.6 us
    all_to_all x1, waiting for transfers between devices, summed_on_arrival(): blocks = lax.all_to_all(cut_along(array, dim, size), axis, 0, 0, tiled=True)  22.3 us
  transfers between devices with their start and end apart: 6, of which 6 were waited for; matrix products, arithmetic and copies ran while one was open for 16% of the time, Pallas kernels for 0%

commit v1 on v0

--- a/solution.py
+++ b/solution.py
@@ -6,6 +6,19 @@
 HEAD_DIM = 128
 TOK_FRAME = 256
 FR_DEV = 2
+
+
+def gather_around(array, axis, dim):
+    ways = lax.axis_size(axis)
+    up = [(d, (d + 1) % ways) for d in range(ways)]
+    down = [(d, (d - 1) % ways) for d in range(ways)]
+    earlier, later = ([array], [array])
+    for _ in range(ways // 2):
+        earlier.append(lax.ppermute(earlier[-1], axis, up))
+    for _ in range((ways - 1) // 2):
+        later.append(lax.ppermute(later[-1], axis, down))
+    line = jnp.concatenate([*earlier[::-1], *later[1:]], axis=dim)
+    return jnp.roll(line, (lax.axis_index(axis) - ways // 2) * array.shape[dim], axis=dim)
 
 
 def laid_out(blocks, dim):
@@ -122,7 +135,7 @@
     query_frame = (seq_index * block + jnp.arange(block, dtype=jnp.int32)) // TOK_FRAME
     peak = jnp.full((local_heads, block), -1e30, jnp.float32)
     key_piece = lax.all_gather(qkv[:, 1], "seq", axis=0, tiled=True)
-    value_piece = lax.all_gather(qkv[:, 2], "seq", axis=0, tiled=True)
+    value_piece = gather_around(qkv[:, 2], "seq", 0)
     width = key_piece.shape[0]
     key_heads = key_piece.reshape(width, local_heads, HEAD_DIM)
     value_heads = value_piece.reshape(width, local_heads, HEAD_DIM)

time: 399 us -> 495 us (1.24); the launches traced: 398 us -> 486 us
  local copies, waits for them, and re-layouts: 6.76 us -> 63.7 us
  starting transfers between devices: 23.7 us -> 77.1 us
  waiting for transfers between devices: 131 us -> 113 us
  blocking collectives: 85.5 us -> 79.2 us
    ppermute x0 -> x15, waiting for transfers between devices: none -> 82.7 us  [the longest x8 67.8 us: gather_around(): earlier.append(lax.ppermute(earlier[-1], axis, up))]
    all_gather x1, waiting for transfers between devices: 69.6 us -> 0.01 us  [local(): key_piece = lax.all_gather(qkv[:, 1], 'seq', axis=0, tiled=True)]
    ppermute x0 -> x15, starting transfers between devices: none -> 49.6 us  [the longest x7 36.9 us: gather_around(): later.append(lax.ppermute(later[-1], axis, down))]
    unnamed x20 -> x77, local copies, waits for them, and re-layouts: 1.8 us -> 50.1 us
    all_gather x1 -> x0, waiting for transfers between devices: 25 us -> none  [local(): value_piece = lax.all_gather(qkv[:, 2], 'seq', axis=0, tiled=True)]
    dynamic_slice x0 -> x1, local copies, waits for them, and re-layouts: none -> 7.68 us  [gather_around(): jnp.roll(line, (lax.axis_index(axis) - ways // 2) * array.shape[dim], axi...]
    all_to_all x1, waiting for transfers between devices: 22.3 us -> 17 us  [summed_on_arrival(): blocks = lax.all_to_all(cut_along(array, dim, size), axis, 0, 0, tiled=True)]
    all_to_all x2, blocking collectives: 57.6 us -> 52.5 us  [sent_to_all(): return lax.all_to_all(copies, axis, split_axis=0, concat_axis=0, tiled=True)]
  transfers between devices with their start and end apart: 6 -> 20, of which waited for: 6 -> 17; matrix products, arithmetic and copies ran while one was open for 16% -> 14% of each run, Pallas kernels for 0% -> 0%
where the time goes in v1:
time: 495 us; the launch traced here: 486 us
  waiting for transfers between devices  113 us (23%)
  matrix products  83.4 us (17%)
  blocking collectives  79.2 us (16%)
  starting transfers between devices  77.1 us (16%)
  local copies, waits for them, and re-layouts  63.7 us (13%)
  other arithmetic  52 us (11%)
  between operations  17.4 us (4%)
    ppermute x8, waiting for transfers between devices, gather_around(): earlier.append(lax.ppermute(earlier[-1], axis, up))  67.8 us
    all_to_all x2, blocking collectives, sent_to_all(): return lax.all_to_all(copies, axis, split_axis=0, concat_axis=0, tiled=True)  52.5 us
    unnamed x77, local copies, waits for them, and re-layouts  50.1 us
    ppermute x7, starting transfers between devices, gather_around(): later.append(lax.ppermute(later[-1], axis, down))  36.9 us
    dot_general x1, matrix products, local(): jnp.einsum('qhe,khe->hqk', query, key_heads, preferred_element_type=jnp.f...  29 us
    dot_general x1, matrix products, local(): jnp.einsum('hqk,khe->hqe', weights.astype(jnp.bfloat16), value_heads, pre...  29 us
    all_to_all x1, blocking collectives, summed_on_arrival(): blocks = lax.all_to_all(cut_along(array, dim, size), axis, 0, 0, tiled=True)  26.7 us
    all_to_all x3, starting transfers between devices, sent_to_all(): return lax.all_to_all(copies, axis, split_axis=0, concat_axis=0, tiled=True)  23 us
  transfers between devices with their start and end apart: 20, of which 17 were waited for; matrix products, arithmetic and copies ran while one was open for 14% of the time, Pallas kernels for 0%

profile of v1, /device:TPU:1, one launch (start us, length us, event | category | flops | bytes accessed | tf_op | source)
XLA Modules:
  0.0 486.0 jit_solution(5691042466854007468)
XLA Ops:
  10.1 31.1 %all_to_all.35 = bf16[4,128,2048]{2,1,0:T(8,128)(2,1)S(1)} all-to-all(bf16[4,128,2048]{2,1,0:T(8,128)(2,1)S(1)} %broadcast_in_dim.104), channel_id=1, replica_groups=mesh['dp'=2,'seq'=16,'tensor'=4] {'tensor'}, dimensions={0} | all-to-all | bytes 4194304 | tf_op jit(solution)/shard_map/all_to_all | solution.py:32
  41.2 6.3 %convolution_convert_fusion.2 = bf16[512,3,512]{0,2,1:T(8,128)(2,1)S(1)} fusion(bf16[512,2048,1]{1,0,2:T(8,128)(2,1)S(1)} %bitcast.77, bf16[3,2048,512]{2,1,0:T(8,128)(2,1)} %param.13), kind=kOutput, calls=%fused_computation.25 | convolution fusion | flops 3222011904 | bytes 9961472 | tf_op jit(solution)/shard_map/nd,cde->nce/dot_general | solution.py:127
  51.1 14.1 %collective-permute-done = bf16[512,512]{0,1:T(8,128)(2,1)S(1)} collective-permute-done((bf16[512,512]{0,1:T(8,128)(2,1)S(1)}, bf16[512,512]{0,1:T(8,128)(2,1)S(1)}, u32[]{:S(2)}, u32[]{:S(2)}) %collective-permute-start) | collective-permute-done | bytes 524320 | tf_op jit(solution)/shard_map/ppermute | solution.py:17
  65.2 4.8 collective-permute-start.8
  70.0 13.6 %collective-permute-done.1 = bf16[512,512]{0,1:T(8,128)(2,1)S(1)} collective-permute-done((bf16[512,512]{0,1:T(8,128)(2,1)S(1)}, bf16[512,512]{0,1:T(8,128)(2,1)S(1)}, u32[]{:S(2)}, u32[]{:S(2)}) %collective-permute-start.1) | collective-permute-done | bytes 524320 | tf_op jit(solution)/shard_map/ppermute | solution.py:17
  84.4 5.4 %collective-permute-start.9 = (bf16[512,512]{0,1:T(8,128)(2,1)S(1)}, bf16[512,512]{0,1:T(8,128)(2,1)S(1)}, u32[]{:S(2)}, u32[]{:S(2)}) collective-permute-start(bf16[512,512]{0,1:T(8,128)(2,1)S(1)} %collective-permute-done.8), channel_id=1, source_target_pairs={{0,60},{4,0},{8,4},{12,8},{16,12},{20,16},{24,20},{28,24},{32,28},... | collective-permute-start | bytes 1572872 | tf_op jit(solution)/shard_map/ppermute | solution.py:19
  89.8 5.6 %collective-permute-done.2 = bf16[512,512]{0,1:T(8,128)(2,1)S(1)} collective-permute-done((bf16[512,512]{0,1:T(8,128)(2,1)S(1)}, bf16[512,512]{0,1:T(8,128)(2,1)S(1)}, u32[]{:S(2)}, u32[]{:S(2)}) %collective-permute-start.2) | collective-permute-done | bytes 524320 | tf_op jit(solution)/shard_map/ppermute | solution.py:17
  97.4 5.5 %collective-permute-start.10 = (bf16[512,512]{0,1:T(8,128)(2,1)S(1)}, bf16[512,512]{0,1:T(8,128)(2,1)S(1)}, u32[]{:S(2)}, u32[]{:S(2)}) collective-permute-start(bf16[512,512]{0,1:T(8,128)(2,1)S(1)} %collective-permute-done.9), channel_id=1, source_target_pairs={{0,60},{4,0},{8,4},{12,8},{16,12},{20,16},{24,20},{28,24},{32,28},... | collective-permute-start | bytes 1572872 | tf_op jit(solution)/shard_map/ppermute | solution.py:19
  102.9 3.8 collective-permute-done.3
  109.6 5.5 %collective-permute-start.11 = (bf16[512,512]{0,1:T(8,128)(2,1)S(1)}, bf16[512,512]{0,1:T(8,128)(2,1)}, u32[]{:S(2)}, u32[]{:S(2)}) collective-permute-start(bf16[512,512]{0,1:T(8,128)(2,1)S(1)} %collective-permute-done.10), channel_id=1, source_target_pairs={{0,60},{4,0},{8,4},{12,8},{16,12},{20,16},{24,20},{28,24},{32,28},... | collective-permute-start | bytes 1572872 | tf_op jit(solution)/shard_map/ppermute | solution.py:19
  121.3 5.3 %collective-permute-start.12 = (bf16[512,512]{0,1:T(8,128)(2,1)}, bf16[512,512]{0,1:T(8,128)(2,1)}, u32[]{:S(2)}, u32[]{:S(2)}) collective-permute-start(bf16[512,512]{0,1:T(8,128)(2,1)} %collective-permute-done.11), channel_id=1, source_target_pairs={{0,60},{4,0},{8,4},{12,8},{16,12},{20,16},{24,20},{28,24},{32,28},... | collective-permute-start | bytes 1572872 | tf_op jit(solution)/shard_map/ppermute | solution.py:19
  126.6 5.1 %collective-permute-done.5 = bf16[512,512]{0,1:T(8,128)(2,1)} collective-permute-done((bf16[512,512]{0,1:T(8,128)(2,1)S(1)}, bf16[512,512]{0,1:T(8,128)(2,1)}, u32[]{:S(2)}, u32[]{:S(2)}) %collective-permute-start.5) | collective-permute-done | bytes 524320 | tf_op jit(solution)/shard_map/ppermute | solution.py:17
  133.0 6.6 %collective-permute-done.12 = bf16[512,512]{0,1:T(8,128)(2,1)} collective-permute-done((bf16[512,512]{0,1:T(8,128)(2,1)}, bf16[512,512]{0,1:T(8,128)(2,1)}, u32[]{:S(2)}, u32[]{:S(2)}) %collective-permute-start.12) | collective-permute-done | bytes 524320 | tf_op jit(solution)/shard_map/ppermute | solution.py:19
  139.6 5.5 %collective-permute-start.13 = (bf16[512,512]{0,1:T(8,128)(2,1)}, bf16[512,512]{0,1:T(8,128)(2,1)}, u32[]{:S(2)}, u32[]{:S(2)}) collective-permute-start(bf16[512,512]{0,1:T(8,128)(2,1)} %collective-permute-done.12), channel_id=1, source_target_pairs={{0,60},{4,0},{8,4},{12,8},{16,12},{20,16},{24,20},{28,24},{32,28},... | collective-permute-start | bytes 1572872 | tf_op jit(solution)/shard_map/ppermute | solution.py:19
  145.1 12.8 %collective-permute-done.6 = bf16[512,512]{0,1:T(8,128)(2,1)} collective-permute-done((bf16[512,512]{0,1:T(8,128)(2,1)}, bf16[512,512]{0,1:T(8,128)(2,1)}, u32[]{:S(2)}, u32[]{:S(2)}) %collective-permute-start.6) | collective-permute-done | bytes 524320 | tf_op jit(solution)/shard_map/ppermute | solution.py:17
  157.9 11.4 %collective-permute-start.7 = (bf16[512,512]{0,1:T(8,128)(2,1)}, bf16[512,512]{0,1:T(8,128)(2,1)}, u32[]{:S(2)}, u32[]{:S(2)}) collective-permute-start(bf16[512,512]{0,1:T(8,128)(2,1)} %collective-permute-done.6), channel_id=1, source_target_pairs={{0,4},{4,8},{8,12},{12,16},{16,20},{20,24},{24,28},{28,32},{32,36}... | collective-permute-start | bytes 1572872 | tf_op jit(solution)/shard_map/ppermute | solution.py:17
  169.3 4.9 %compare_and_fusion = pred[512,8192]{1,0:T(8,128)(4,1)} fusion(s32[8192]{0:T(1024)S(1)} %add_select_fusion, s32[512]{0:T(512)S(1)} %add_select_fusion.1, pred[8192]{0:T(1024)(128)(4,1)S(1)} %broadcast_compare_fusion), kind=kLoop, calls=%fused_computation.7 | loop fusion | flops 8388608 | bytes 4237312 | tf_op jit(solution)/shard_map/and | solution.py:146
  174.3 4.8 collective-permute-start.14
  179.1 9.3 %collective-permute-done.7 = bf16[512,512]{0,1:T(8,128)(2,1)} collective-permute-done((bf16[512,512]{0,1:T(8,128)(2,1)}, bf16[512,512]{0,1:T(8,128)(2,1)}, u32[]{:S(2)}, u32[]{:S(2)}) %collective-permute-start.7) | collective-permute-done | bytes 524320 | tf_op jit(solution)/shard_map/ppermute | solution.py:17
  236.4 7.7 %constant_dynamic-slice_fusion = bf16[8192,512]{0,1:T(8,128)(2,1)} fusion(bf16[16384,512]{0,1:T(8,128)(2,1)} %constant_dynamic-update-slice_fusion, s32[]{:T(128)S(6)} %select_n.125), kind=kLoop, calls=%fused_computation.150 | loop fusion | bytes 16777220 | tf_op jit(solution)/shard_map/jit(_roll_dynamic)/dynamic_slice | solution.py:21
  244.1 29.0 %fusion = (f32[4,512]{1,0:T(4,128)S(1)}, f32[4,512,8192]{2,1,0:T(8,128)}) fusion(pred[512,8192]{1,0:T(8,128)(4,1)} %compare_and_fusion, bf16[512,4,128]{0,2,1:T(8,128)(2,1)} %bitcast.80, bf16[8192,4,128]{0,2,1:T(8,128)(2,1)} %bitcast.85), kind=kOutput, calls=%fused_computation.2 | convolution fusion | flops 4345296896 | bytes 80224256 | tf_op jit(solution)/shard_map/qhe,khe->hqk/dot_general | solution.py:143
  273.1 22.9 %fusion.1 = f32[4,512]{1,0:T(4,128)S(1)} fusion(f32[4,512,8192]{2,1,0:T(8,128)} %get-tuple-element.36, f32[4,512]{1,0:T(4,128)S(1)} %broadcast_maximum_fusion, pred[512,8192]{1,0:T(8,128)(4,1)} %compare_and_fusion), kind=kLoop, calls=%fused_computation.3 | loop fusion | flops 83884032 | bytes 71319552 | tf_op jit(solution)/shard_map/reduce_sum | solution.py:150
  296.0 29.0 %divide_convert_fusion = bf16[512,4,128]{0,2,1:T(8,128)(2,1)S(1)} fusion(bf16[8192,4,128]{0,2,1:T(8,128)(2,1)} %bitcast.75, f32[4,512,8192]{2,1,0:T(8,128)} %get-tuple-element.36, f32[4,512]{1,0:T(4,128)S(1)} %broadcast_maximum_fusion, pred[512,8192]{1,0:T(8,128)(4,1)} %compare_and_fusion, f32[512,4]{0,1:T(4,128)S(1)} %bitcast.84), kind=kOutput, calls=%fused_computation.46 | convolution fusion | flops 4379377664 | bytes 80232448 | tf_op jit(solution)/shard_map/hqk,khe->hqe/dot_general | solution.py:151
  326.3 26.7 %all_to_all.36 = bf16[4,128,2048]{2,1,0:T(8,128)(2,1)S(1)} all-to-all(bf16[4,128,2048]{2,1,0:T(8,128)(2,1)S(1)} %bitcast.78), channel_id=1, replica_groups=mesh['dp'=2,'seq'=16,'tensor'=4] {'tensor'}, dimensions={0} | all-to-all | bytes 4194304 | tf_op jit(solution)/shard_map/all_to_all | solution.py:47
  355.9 21.4 %all_to_all.37 = bf16[4,128,2048]{2,1,0:T(8,128)(2,1)} all-to-all(bf16[4,128,2048]{2,1,0:T(8,128)(2,1)S(1)} %broadcast_in_dim.108), channel_id=1, replica_groups=mesh['dp'=2,'seq'=16,'tensor'=4] {'tensor'}, dimensions={0} | all-to-all | bytes 4194304 | tf_op jit(solution)/shard_map/all_to_all | solution.py:32
  377.3 16.6 %convolution_convert_fusion = bf16[512,2048]{1,0:T(8,128)(2,1)} fusion(bf16[2048,2048]{1,0:T(8,128)(2,1)} %param.17, bf16[512,2048]{1,0:T(8,128)(2,1)} %bitcast.79, bf16[2048,2048]{1,0:T(8,128)(2,1)} %param.16), kind=kOutput, calls=%fused_computation.19 | convolution fusion | flops 8600420352 | bytes 20971520 | tf_op jit(solution)/shard_map/dot_general | solution.py:174
  393.9 4.4 all-to-all-start.3
  398.4 17.0 %all-to-all-done.3 = bf16[4,128,2048]{2,1,0:T(8,128)(2,1)} async-done(((bf16[4,128,2048]{2,1,0:T(8,128)(2,1)}), bf16[4,128,2048]{2,1,0:T(8,128)(2,1)}, u32[]{:S(2)}, u32[]{:S(2)}) %all-to-all-start.3) | async-done | bytes 2097184 | tf_op jit(solution)/shard_map/all_to_all | solution.py:47
  424.4 3.8 all-to-all-done.4
  435.8 5.0 %all-to-all-done.5 = f32[16,2,2048]{2,1,0:T(2,128)S(1)} async-done(((f32[16,2,2048]{2,1,0:T(2,128)}), f32[16,2,2048]{2,1,0:T(2,128)S(1)}, u32[]{:S(2)}, u32[]{:S(2)}) %all-to-all-start.5) | async-done | bytes 262176 | tf_op jit(solution)/shard_map/all_to_all | solution.py:32
  449.7 16.1 %all-to-all-start.6 = ((f32[32,3,2]{1,2,0:T(2,128)}), f32[32,3,2]{1,2,0:T(2,128)S(1)}, u32[]{:S(2)}, u32[]{:S(2)}) async-start(f32[32,3,2]{1,2,0:T(2,128)} %broadcast_in_dim.118), calls=%async_computation.6 | async-start | bytes 65536 | tf_op jit(solution)/shard_map/all_to_all | solution.py:32
  468.2 4.7 all-to-all-done.6
  (156 shorter events, 102.7 us)
Async XLA Ops:
  7.2 317.8 %copy-start = (bf16[512,2048]{1,0:T(8,128)(2,1)S(1)}, bf16[512,2048]{1,0:T(8,128)(2,1)}, u32[]{:S(2)}) copy-start(bf16[512,2048]{1,0:T(8,128)(2,1)} %param.14) | copy-start | bytes 6291460
  7.2 236.9 %all-gather.3.cloned.1.call-start = ((), (), s32[]{:S(2)}) async-start(), calls=%async_computation.7 | async-start | bytes 8912896 | tf_op jit(solution)/shard_map/all_gather | solution.py:137
  41.2 90.5 %copy-start.21 = (s32[2]{0:T(128)S(1)}, s32[2]{0:T(128)}, u32[]{:S(2)}) copy-start(s32[2]{0:T(128)} %param.21) | copy-start | bytes 28
  49.8 15.4 %collective-permute-start = (bf16[512,512]{0,1:T(8,128)(2,1)S(1)}, bf16[512,512]{0,1:T(8,128)(2,1)S(1)}, u32[]{:S(2)}, u32[]{:S(2)}) collective-permute-start(bf16[512,512]{0,1:T(8,128)(2,1)S(1)} %get-tuple-element.21), channel_id=1, source_target_pairs={{0,4},{4,8},{8,12},{12,16},{16,20},{20,24},{24,28},{28,32},{32,36}... | collective-permute-start | bytes 1572872 | tf_op jit(solution)/shard_map/ppermute | solution.py:17
  65.2 18.4 %collective-permute-start.1 = (bf16[512,512]{0,1:T(8,128)(2,1)S(1)}, bf16[512,512]{0,1:T(8,128)(2,1)S(1)}, u32[]{:S(2)}, u32[]{:S(2)}) collective-permute-start(bf16[512,512]{0,1:T(8,128)(2,1)S(1)} %collective-permute-done), channel_id=1, source_target_pairs={{0,4},{4,8},{8,12},{12,16},{16,20},{20,24},{24,28},{28,32},{32,36}... | collective-permute-start | bytes 1572872 | tf_op jit(solution)/shard_map/ppermute | solution.py:17
  65.2 19.2 %collective-permute-start.8 = (bf16[512,512]{0,1:T(8,128)(2,1)}, bf16[512,512]{0,1:T(8,128)(2,1)S(1)}, u32[]{:S(2)}, u32[]{:S(2)}) collective-permute-start(bf16[512,512]{0,1:T(8,128)(2,1)} %copy-done.16), channel_id=1, source_target_pairs={{0,60},{4,0},{8,4},{12,8},{16,12},{20,16},{24,20},{28,24},{32,28},... | collective-permute-start | bytes 1572872 | tf_op jit(solution)/shard_map/ppermute | solution.py:19
  83.5 11.9 %collective-permute-start.2 = (bf16[512,512]{0,1:T(8,128)(2,1)S(1)}, bf16[512,512]{0,1:T(8,128)(2,1)S(1)}, u32[]{:S(2)}, u32[]{:S(2)}) collective-permute-start(bf16[512,512]{0,1:T(8,128)(2,1)S(1)} %collective-permute-done.1), channel_id=1, source_target_pairs={{0,4},{4,8},{8,12},{12,16},{16,20},{20,24},{24,28},{28,32},{32,36}... | collective-permute-start | bytes 1572872 | tf_op jit(solution)/shard_map/ppermute | solution.py:17
  84.4 13.0 %collective-permute-start.9 = (bf16[512,512]{0,1:T(8,128)(2,1)S(1)}, bf16[512,512]{0,1:T(8,128)(2,1)S(1)}, u32[]{:S(2)}, u32[]{:S(2)}) collective-permute-start(bf16[512,512]{0,1:T(8,128)(2,1)S(1)} %collective-permute-done.8), channel_id=1, source_target_pairs={{0,60},{4,0},{8,4},{12,8},{16,12},{20,16},{24,20},{28,24},{32,28},... | collective-permute-start | bytes 1572872 | tf_op jit(solution)/shard_map/ppermute | solution.py:19
  95.4 11.4 %collective-permute-start.3 = (bf16[512,512]{0,1:T(8,128)(2,1)S(1)}, bf16[512,512]{0,1:T(8,128)(2,1)S(1)}, u32[]{:S(2)}, u32[]{:S(2)}) collective-permute-start(bf16[512,512]{0,1:T(8,128)(2,1)S(1)} %collective-permute-done.2), channel_id=1, source_target_pairs={{0,4},{4,8},{8,12},{12,16},{16,20},{20,24},{24,28},{28,32},{32,36}... | collective-permute-start | bytes 1572872 | tf_op jit(solution)/shard_map/ppermute | solution.py:17
  97.4 12.2 %collective-permute-start.10 = (bf16[512,512]{0,1:T(8,128)(2,1)S(1)}, bf16[512,512]{0,1:T(8,128)(2,1)S(1)}, u32[]{:S(2)}, u32[]{:S(2)}) collective-permute-start(bf16[512,512]{0,1:T(8,128)(2,1)S(1)} %collective-permute-done.9), channel_id=1, source_target_pairs={{0,60},{4,0},{8,4},{12,8},{16,12},{20,16},{24,20},{28,24},{32,28},... | collective-permute-start | bytes 1572872 | tf_op jit(solution)/shard_map/ppermute | solution.py:19
  106.8 11.9 %collective-permute-start.4 = (bf16[512,512]{0,1:T(8,128)(2,1)S(1)}, bf16[512,512]{0,1:T(8,128)(2,1)S(1)}, u32[]{:S(2)}, u32[]{:S(2)}) collective-permute-start(bf16[512,512]{0,1:T(8,128)(2,1)S(1)} %collective-permute-done.3), channel_id=1, source_target_pairs={{0,4},{4,8},{8,12},{12,16},{16,20},{20,24},{24,28},{28,32},{32,36}... | collective-permute-start | bytes 1572872 | tf_op jit(solution)/shard_map/ppermute | solution.py:17
  109.6 11.6 %collective-permute-start.11 = (bf16[512,512]{0,1:T(8,128)(2,1)S(1)}, bf16[512,512]{0,1:T(8,128)(2,1)}, u32[]{:S(2)}, u32[]{:S(2)}) collective-permute-start(bf16[512,512]{0,1:T(8,128)(2,1)S(1)} %collective-permute-done.10), channel_id=1, source_target_pairs={{0,60},{4,0},{8,4},{12,8},{16,12},{20,16},{24,20},{28,24},{32,28},... | collective-permute-start | bytes 1572872 | tf_op jit(solution)/shard_map/ppermute | solution.py:19
  118.6 13.1 %collective-permute-start.5 = (bf16[512,512]{0,1:T(8,128)(2,1)S(1)}, bf16[512,512]{0,1:T(8,128)(2,1)}, u32[]{:S(2)}, u32[]{:S(2)}) collective-permute-start(bf16[512,512]{0,1:T(8,128)(2,1)S(1)} %collective-permute-done.4), channel_id=1, source_target_pairs={{0,4},{4,8},{8,12},{12,16},{16,20},{20,24},{24,28},{28,32},{32,36}... | collective-permute-start | bytes 1572872 | tf_op jit(solution)/shard_map/ppermute | solution.py:17
  121.3 18.3 %collective-permute-start.12 = (bf16[512,512]{0,1:T(8,128)(2,1)}, bf16[512,512]{0,1:T(8,128)(2,1)}, u32[]{:S(2)}, u32[]{:S(2)}) collective-permute-start(bf16[512,512]{0,1:T(8,128)(2,1)} %collective-permute-done.11), channel_id=1, source_target_pairs={{0,60},{4,0},{8,4},{12,8},{16,12},{20,16},{24,20},{28,24},{32,28},... | collective-permute-start | bytes 1572872 | tf_op jit(solution)/shard_map/ppermute | solution.py:19
  131.7 26.2 %collective-permute-start.6 = (bf16[512,512]{0,1:T(8,128)(2,1)}, bf16[512,512]{0,1:T(8,128)(2,1)}, u32[]{:S(2)}, u32[]{:S(2)}) collective-permute-start(bf16[512,512]{0,1:T(8,128)(2,1)} %collective-permute-done.5), channel_id=1, source_target_pairs={{0,4},{4,8},{8,12},{12,16},{16,20},{20,24},{24,28},{28,32},{32,36}... | collective-permute-start | bytes 1572872 | tf_op jit(solution)/shard_map/ppermute | solution.py:17
  139.6 34.7 %collective-permute-start.13 = (bf16[512,512]{0,1:T(8,128)(2,1)}, bf16[512,512]{0,1:T(8,128)(2,1)}, u32[]{:S(2)}, u32[]{:S(2)}) collective-permute-start(bf16[512,512]{0,1:T(8,128)(2,1)} %collective-permute-done.12), channel_id=1, source_target_pairs={{0,60},{4,0},{8,4},{12,8},{16,12},{20,16},{24,20},{28,24},{32,28},... | collective-permute-start | bytes 1572872 | tf_op jit(solution)/shard_map/ppermute | solution.py:19
  157.9 30.5 %collective-permute-start.7 = (bf16[512,512]{0,1:T(8,128)(2,1)}, bf16[512,512]{0,1:T(8,128)(2,1)}, u32[]{:S(2)}, u32[]{:S(2)}) collective-permute-start(bf16[512,512]{0,1:T(8,128)(2,1)} %collective-permute-done.6), channel_id=1, source_target_pairs={{0,4},{4,8},{8,12},{12,16},{16,20},{20,24},{24,28},{28,32},{32,36}... | collective-permute-start | bytes 1572872 | tf_op jit(solution)/shard_map/ppermute | solution.py:17
  174.2 46.9 %copy-start.15 = (bf16[512,512]{0,1:T(8,128)(2,1)S(1)}, bf16[512,512]{0,1:T(8,128)(2,1)}, u32[]{:S(2)}) copy-start(bf16[512,512]{0,1:T(8,128)(2,1)} %copy-done.14) | copy-start | bytes 1572868
  174.2 47.8 %copy-start.13 = (bf16[512,512]{0,1:T(8,128)(2,1)S(1)}, bf16[512,512]{0,1:T(8,128)(2,1)}, u32[]{:S(2)}) copy-start(bf16[512,512]{0,1:T(8,128)(2,1)} %copy-done.12) | copy-start | bytes 1572868
  174.2 48.6 %copy-start.9 = (bf16[512,512]{0,1:T(8,128)(2,1)S(1)}, bf16[512,512]{0,1:T(8,128)(2,1)}, u32[]{:S(2)}) copy-start(bf16[512,512]{0,1:T(8,128)(2,1)} %copy-done.8) | copy-start | bytes 1572868
  174.2 49.5 %copy-start.5 = (bf16[512,512]{0,1:T(8,128)(2,1)S(1)}, bf16[512,512]{0,1:T(8,128)(2,1)}, u32[]{:S(2)}) copy-start(bf16[512,512]{0,1:T(8,128)(2,1)} %copy-done.4) | copy-start | bytes 1572868
  174.2 53.9 %copy-start.7 = (bf16[512,512]{0,1:T(8,128)(2,1)S(1)}, bf16[512,512]{0,1:T(8,128)(2,1)}, u32[]{:S(2)}) copy-start(bf16[512,512]{0,1:T(8,128)(2,1)} %copy-done.6) | copy-start | bytes 1572868
  174.2 54.7 %copy-start.11 = (bf16[512,512]{0,1:T(8,128)(2,1)S(1)}, bf16[512,512]{0,1:T(8,128)(2,1)}, u32[]{:S(2)}) copy-start(bf16[512,512]{0,1:T(8,128)(2,1)} %copy-done.10) | copy-start | bytes 1572868
  174.3 40.4 %collective-permute-start.14 = (bf16[512,512]{0,1:T(8,128)(2,1)}, bf16[512,512]{0,1:T(8,128)(2,1)S(1)}, u32[]{:S(2)}, u32[]{:S(2)}) collective-permute-start(bf16[512,512]{0,1:T(8,128)(2,1)} %collective-permute-done.13), channel_id=1, source_target_pairs={{0,60},{4,0},{8,4},{12,8},{16,12},{20,16},{24,20},{28,24},{32,28},... | collective-permute-start | bytes 1572872 | tf_op jit(solution)/shard_map/ppermute | solution.py:19
  296.0 59.5 %copy-start.18 = (f32[2048]{0:T(1024)S(1)}, f32[2048]{0:T(1024)}, u32[]{:S(2)}) copy-start(f32[2048]{0:T(1024)} %param.15) | copy-start | bytes 24580
  377.3 21.1 %copy-start.19 = (f32[2048]{0:T(1024)S(1)}, f32[2048]{0:T(1024)}, u32[]{:S(2)}) copy-start(f32[2048]{0:T(1024)} %param.18) | copy-start | bytes 24580
  377.3 50.9 %copy-start.20 = (f32[2048]{0:T(1024)S(1)}, f32[2048]{0:T(1024)}, u32[]{:S(2)}) copy-start(f32[2048]{0:T(1024)} %param.19) | copy-start | bytes 24580
  377.3 56.0 %copy-start.22 = (s32[2]{0:T(128)S(1)}, s32[2]{0:T(128)}, u32[]{:S(2)}) copy-start(s32[2]{0:T(128)} %param.21) | copy-start | bytes 28
  393.9 21.5 %all-to-all-start.3 = ((bf16[4,128,2048]{2,1,0:T(8,128)(2,1)}), bf16[4,128,2048]{2,1,0:T(8,128)(2,1)}, u32[]{:S(2)}, u32[]{:S(2)}) async-start(bf16[4,128,2048]{2,1,0:T(8,128)(2,1)} %bitcast.76), calls=%async_computation.3 | async-start | bytes 4194304 | tf_op jit(solution)/shard_map/all_to_all | solution.py:47
  420.4 7.7 %all-to-all-start.4 = ((f32[4,2,2048]{2,1,0:T(2,128)}), f32[4,2,2048]{2,1,0:T(2,128)S(1)}, u32[]{:S(2)}, u32[]{:S(2)}) async-start(f32[4,2,2048]{2,1,0:T(2,128)} %broadcast_in_dim.110), calls=%async_computation.4 | async-start | bytes 131072 | tf_op jit(solution)/shard_map/all_to_all | solution.py:32
  429.8 11.0 %all-to-all-start.5 = ((f32[16,2,2048]{2,1,0:T(2,128)}), f32[16,2,2048]{2,1,0:T(2,128)S(1)}, u32[]{:S(2)}, u32[]{:S(2)}) async-start(f32[16,2,2048]{2,1,0:T(2,128)} %broadcast_in_dim.113), calls=%async_computation.5 | async-start | bytes 524288 | tf_op jit(solution)/shard_map/all_to_all | solution.py:32
  449.7 23.1 %all-to-all-start.6 = ((f32[32,3,2]{1,2,0:T(2,128)}), f32[32,3,2]{1,2,0:T(2,128)S(1)}, u32[]{:S(2)}, u32[]{:S(2)}) async-start(f32[32,3,2]{1,2,0:T(2,128)} %broadcast_in_dim.118), calls=%async_computation.6 | async-start | bytes 65536 | tf_op jit(solution)/shard_map/all_to_all | solution.py:32
  (11 other events, 81.5 us)
Sparse Core Ops, SparseCore 0:
  49.9 140.6 all-gather.2
